TPU v7x, 32 devices: a whole 2x2x4 slice. The times are simulated.
32 devices in a mesh: ep: 16 (over z, y, core), dp: 2 (over x).
Axes of the slice: x: 2, y: 2, z: 4, core: 2. Of those that a mesh axis runs over, the one named last changes fastest.
Arguments:
- tokens: bfloat16 [512, 3584], P(('ep', 'dp')), may hold values from -6 to 6
- norm_gain: float32 [3584], replicated, may hold values from 0.25 to 1.75
- router: bfloat16 [3584, 16], replicated, may hold values from -0.09375 to 0.09375
- next_router: bfloat16 [3584, 16], P('dp'), may hold values from -0.09375 to 0.09375
- expert_ids: int32 [512, 8], P(('ep', 'dp')), may hold values from 0 to 15, all different within a row; in each aligned block of 16 rows (0 to 15, 16 to 31, ...) at most 16 rows name the same one
- store: bfloat16 [16, 2, 224, 128, 128], P('ep', 'dp'), may hold values from -0.125 to 0.125
- send_list: int32 [16, 224], P('ep'), may hold values from -1 to 223, as said below
- cache_map: int32 [16, 224], P('ep'), may hold values from 0 to 223, as said below
Outputs:
- layer_out: bfloat16 [512, 3584], P(('ep', 'dp'))
- next_scores: float32 [512, 16], P(('ep', 'dp'))
Inputs may be any that keep to these rules, and one draw needn't show every extreme that they name: `expert_ids`: each row names 8 different experts; among the rows of one device no expert is named by more than 16 rows, a bound that some block reaches. `send_list`: an entry is -1 where that arriving slot stays empty; every row names each of the 224 store indices exactly once. `cache_map`: each entry numbers an arriving slot of that device that is never empty; the entries of a row are distinct.
All inputs are finite; a program needn't handle non-finite values.
Results may differ from a plain program's by a relative error of at most 0.0095.
Values may be sent and summed in bfloat16 or wider, within the bound.
No kernel may reach another device: no remote copies, remote signals or barrier semaphores. Data moves between devices by JAX's collectives and lax.ppermute only.
A program may use at most 64 MiB of HBM per device.

v0:
```python
import jax
import jax.numpy as jnp
from jax import lax
from jax.sharding import PartitionSpec as P


def per_device(tokens, norm_gain, router, next_router, expert_ids, store, send_list, cache_map):
    tok_dev, width = tokens.shape
    n_dp = lax.axis_size("dp")
    experts = router.shape[1]
    top = expert_ids.shape[1]
    tiles = cache_map.shape[1]
    tile_rows = store.shape[3]
    tile_cols = store.shape[4]
    part = width // n_dp
    row_tiles = part // tile_rows
    col_tiles = tiles // (2 * row_tiles)
    hidden_width = col_tiles * tile_cols
    capacity = min(tok_dev, max(2, 2 * tok_dev * top // experts))
    values = tokens.astype(jnp.float32)
    scale = lax.rsqrt(jnp.mean(values * values, axis=1, keepdims=True) + 1e-06)
    normed = (values * scale * norm_gain).astype(jnp.bfloat16)
    scores = jax.nn.sigmoid(jnp.dot(normed, router, preferred_element_type=jnp.float32))
    chosen = (expert_ids[:, :, None] == jnp.arange(experts, dtype=jnp.int32)[None, None, :]).astype(
        jnp.float32
    )
    picked = jnp.sum(chosen * scores[:, None, :], axis=2)
    weights = (2.5 * picked / jnp.sum(picked, axis=1, keepdims=True)).astype(jnp.bfloat16)
    flat = chosen.reshape(tok_dev * top, experts)
    before = jnp.cumsum(flat, axis=0) - flat
    rank = jnp.sum(before * flat, axis=1).astype(jnp.int32)
    slot = expert_ids.reshape(-1) * capacity + rank
    columns = jnp.arange(experts * capacity, dtype=jnp.int32)
    match = (slot[:, None] == columns[None, :]).reshape(tok_dev, top, experts * capacity)
    dispatch = jnp.sum(match.astype(jnp.float32), axis=1).astype(jnp.bfloat16)
    combine = jnp.sum(
        jnp.where(match, weights.astype(jnp.float32)[:, :, None], 0.0), axis=1
    ).astype(jnp.bfloat16)
    outgoing = lax.dot_general(
        dispatch, normed, (((0,), (0,)), ((), ())), preferred_element_type=jnp.float32
    ).astype(jnp.bfloat16)
    owned = store.reshape(tiles, tile_rows, tile_cols)
    wanted = send_list.reshape(-1)
    present = wanted >= 0
    leaving = jnp.where(
        present[:, None, None], owned[jnp.maximum(wanted, 0)], jnp.zeros((), jnp.bfloat16)
    )
    arrived = lax.all_to_all(leaving, "ep", split_axis=0, concat_axis=0, tiled=True)
    cached = arrived[cache_map.reshape(-1)].reshape(2, row_tiles, col_tiles, tile_rows, tile_cols)
    up_tiles = cached[0]
    down_tiles = cached[1]
    rows = lax.all_to_all(
        lax.all_to_all(outgoing, "ep", split_axis=0, concat_axis=0, tiled=True),
        "dp",
        split_axis=1,
        concat_axis=0,
        tiled=True,
    )
    count = rows.shape[0]
    block = rows.reshape(count, row_tiles, tile_rows)
    product = jnp.einsum("nat,acts->ncs", block, up_tiles, preferred_element_type=jnp.float32)
    summed = lax.psum(product.reshape(count, hidden_width).astype(jnp.bfloat16), "dp").astype(
        jnp.float32
    )
    hidden = jax.nn.silu(summed).astype(jnp.bfloat16)
    number = hidden.shape[0]
    product = jnp.einsum(
        "ncs,acts->nat",
        hidden.reshape(number, col_tiles, tile_cols),
        down_tiles,
        preferred_element_type=jnp.float32,
    )
    result = product.reshape(number, part).astype(jnp.bfloat16)
    back = lax.all_to_all(
        lax.all_to_all(result, "dp", split_axis=0, concat_axis=1, tiled=True),
        "ep",
        split_axis=0,
        concat_axis=0,
        tiled=True,
    )
    mixed = jnp.dot(combine, back, preferred_element_type=jnp.float32)
    layer_out = (values + mixed).astype(jnp.bfloat16)
    stream = layer_out.astype(jnp.float32)
    renorm = lax.rsqrt(jnp.mean(stream * stream, axis=1, keepdims=True) + 1e-06)
    next_normed = (stream * renorm).astype(jnp.bfloat16)
    features = lax.all_to_all(next_normed, "dp", split_axis=1, concat_axis=0, tiled=True)
    partial_scores = jnp.dot(features, next_router, preferred_element_type=jnp.float32)
    next_logits = lax.psum_scatter(
        partial_scores.astype(jnp.bfloat16), "dp", scatter_dimension=0, tiled=True
    ).astype(jnp.float32)
    return (layer_out, jax.nn.sigmoid(next_logits))


def solution(mesh):
    in_specs = (
        P(("ep", "dp"), None),
        P(),
        P(),
        P("dp", None),
        P(("ep", "dp"), None),
        P("ep", "dp", None, None, None),
        P("ep", None),
        P("ep", None),
    )
    out_specs = (P(("ep", "dp"), None), P(("ep", "dp"), None))
    return jax.shard_map(
        per_device, mesh=mesh, in_specs=in_specs, out_specs=out_specs, check_vma=False
    )
```

profile of v0, /device:TPU:0, one launch (start us, length us, event | category | flops | bytes accessed | tf_op | source)
XLA Modules:
  0.0 437.3 jit_solution(8908242254397563168)
XLA Ops:
  7.2 0.0 copy-start
  7.2 0.0 copy-start.6
  7.2 1.1 fusion.17
  8.3 0.8 copy.46
  9.0 0.1 eq.36
  9.1 0.0 copy-done
  9.1 1.1 fusion.11
  10.3 0.3 select_reduce_fusion.1
  10.6 0.1 fusion.20
  10.7 0.2 reduce_window_sum.11
  10.9 0.2 select_reduce_fusion.3
  11.0 0.1 convert_element_type.76
  11.1 0.1 fusion.25
  11.2 0.2 select_reduce_fusion
  11.4 2.9 convolution_convert_fusion
  14.3 7.4 %all-to-all-start = ((bf16[16,16,3584]{2,1,0:T(8,128)(2,1)}), bf16[16,16,3584]{2,1,0:T(8,128)(2,1)S(1)}, u32[]{:S(2)}, u32[]{:S(2)}) async-start(bf16[16,16,3584]{2,1,0:T(8,128)(2,1)} %bitcast.49), calls=%async_computation | async-start | bytes 3670016 | tf_op jit(solution)/shard_map/all_to_all | solution.py:53
  21.7 0.0 copy-done.6
  21.8 11.5 %gather_fusion = bf16[224,128,128]{2,1,0:T(8,128)(2,1)} fusion(bf16[224,128,128]{2,1,0:T(8,128)(2,1)} %bitcast.50, s32[1024]{0:T(1024)S(1)} %pad_clamp_fusion.1), kind=kCustom, calls=%fused_computation | custom fusion | bytes 14680960 | tf_op jit(solution)/shard_map/gather | solution.py:46
  33.2 24.9 %all-to-all-done = bf16[16,16,3584]{2,1,0:T(8,128)(2,1)S(1)} async-done(((bf16[16,16,3584]{2,1,0:T(8,128)(2,1)}), bf16[16,16,3584]{2,1,0:T(8,128)(2,1)S(1)}, u32[]{:S(2)}, u32[]{:S(2)}) %all-to-all-start) | async-done | bytes 1835040 | tf_op jit(solution)/shard_map/all_to_all | solution.py:53
  58.1 1.5 all_to_all.57
  59.6 3.0 copy.49
  62.6 3.7 all-to-all-start.1
  66.3 6.6 %broadcast_select_fusion = bf16[224,128,128]{2,1,0:T(8,128)(2,1)} fusion(bf16[224,128,128]{2,1,0:T(8,128)(2,1)} %gather_fusion, pred[224]{0:T(512)(128)(4,1)S(1)} %compare_reduce_fusion), kind=kLoop, calls=%fused_computation.2 | loop fusion | flops 3670016 | bytes 14680288 | tf_op jit(solution)/shard_map/jit(_where)/select_n | solution.py:45
  73.0 0.0 copy-start.7
  73.0 16.8 %all-to-all-done.1 = bf16[256,2,1792]{2,0,1:T(8,128)(2,1)S(1)} async-done(((bf16[256,2,1792]{2,0,1:T(8,128)(2,1)}), bf16[256,2,1792]{2,0,1:T(8,128)(2,1)S(1)}, u32[]{:S(2)}, u32[]{:S(2)}) %all-to-all-start.1) | async-done | bytes 1835040 | tf_op jit(solution)/shard_map/all_to_all | solution.py:52
  89.7 9.6 %all-to-all-start.2 = ((bf16[224,128,128]{2,1,0:T(8,128)(2,1)}), bf16[224,128,128]{2,1,0:T(8,128)(2,1)}, u32[]{:S(2)}, u32[]{:S(2)}) async-start(bf16[224,128,128]{2,1,0:T(8,128)(2,1)} %broadcast_select_fusion), calls=%async_computation.2 | async-start | bytes 14680064 | tf_op jit(solution)/shard_map/all_to_all | solution.py:48
  99.4 0.2 all-reduce.2.cloned.1.call-start
  99.6 0.0 copy-done.7
  99.6 2.4 reshape.175
  102.1 129.6 %all-to-all-done.2 = bf16[224,128,128]{2,1,0:T(8,128)(2,1)} async-done(((bf16[224,128,128]{2,1,0:T(8,128)(2,1)}), bf16[224,128,128]{2,1,0:T(8,128)(2,1)}, u32[]{:S(2)}, u32[]{:S(2)}) %all-to-all-start.2) | async-done | bytes 7340064 | tf_op jit(solution)/shard_map/all_to_all | solution.py:48
  231.7 11.4 %gather_fusion.1 = bf16[224,128,128]{2,1,0:T(8,128)(2,1)} fusion(bf16[224,128,128]{2,1,0:T(8,128)(2,1)} %all-to-all-done.2, s32[1024]{0:T(1024)S(1)} %pad_clamp_fusion), kind=kCustom, calls=%fused_computation.1 | custom fusion | bytes 14680960 | tf_op jit(solution)/shard_map/gather | solution.py:49
  243.1 9.4 %fusion.26 = (bf16[112,128,128]{2,1,0:T(8,128)(2,1)}, bf16[112,128,128]{2,1,0:T(8,128)(2,1)}) fusion(bf16[224,128,128]{2,1,0:T(8,128)(2,1)} %gather_fusion.1), kind=kLoop, calls=%fused_computation.56 | loop fusion | bytes 14680064 | tf_op jit(solution)/shard_map/slice | solution.py:50
  252.5 0.0 copy-start.2
  252.5 6.1 %copy.51 = bf16[14,8,128,128]{2,3,1,0:T(8,128)(2,1)} copy(bf16[14,8,128,128]{3,2,1,0:T(8,128)(2,1)} %bitcast.45) | data formatting | bytes 7340032 | tf_op jit(solution)/shard_map/squeeze | solution.py:50
  258.6 0.0 copy-done.2
  258.6 5.1 %bitcast_convert_fusion.1 = bf16[512,1024]{1,0:T(8,128)(2,1)} fusion(bf16[1024,14,128]{2,0,1:T(8,128)(2,1)} %bitcast.52, bf16[512,14,128]{2,1,0:T(8,128)(2,1)S(1)} %copy-done.2), kind=kOutput, calls=%fused_computation.13 | convolution fusion | flops 1879572480 | bytes 6553600 | tf_op jit(solution)/shard_map/nat,acts->ncs/dot_general | solution.py:61
  263.7 0.0 all-reduce.2.cloned.1.call-update
  263.7 0.0 reduce-scatter.2.cloned.1.call-start
  263.7 4.3 copy.53
  268.1 62.6 %all-reduce.2.cloned.1.call-done = bf16[512,1024]{1,0:T(8,128)(2,1)} async-done(((bf16[512,1024]{1,0:T(8,128)(2,1)}), bf16[512,1024]{1,0:T(8,128)(2,1)}) %all-reduce.2.cloned.1.call-update) | async-done | bytes 1048592 | tf_op jit(solution)/shard_map/psum | solution.py:62
  330.6 4.7 %bitcast_convert_fusion = bf16[512,1792]{1,0:T(8,128)(2,1)S(1)} fusion(bf16[1792,8,128]{2,0,1:T(8,128)(2,1)} %bitcast.51, bf16[512,1024]{1,0:T(8,128)(2,1)} %all-reduce.2.cloned.1.call-done), kind=kOutput, calls=%fused_computation.6 | convolution fusion | flops 1883111424 | bytes 6553600 | tf_op jit(solution)/shard_map/ncs,acts->nat/dot_general | solution.py:67
  335.4 24.7 %all_to_all.77 = bf16[2,256,1792]{2,1,0:T(8,128)(2,1)S(1)} all-to-all(bf16[2,256,1792]{2,1,0:T(8,128)(2,1)S(1)} %bitcast.53), channel_id=1, replica_groups=mesh['ep'=16,'dp'=2] {'dp'}, dimensions={0} | all-to-all | bytes 3670016 | tf_op jit(solution)/shard_map/all_to_all | solution.py:75
  360.0 1.9 copy.55
  361.9 0.0 copy-start.3
  361.9 0.0 copy-start.1
  362.0 2.2 all_to_all.64
  364.1 0.0 copy-start.5
  364.1 48.3 %all_to_all.78 = bf16[16,16,3584]{2,1,0:T(8,128)(2,1)S(1)} all-to-all(bf16[16,16,3584]{2,1,0:T(8,128)(2,1)} %all_to_all.64), channel_id=1, replica_groups=mesh['ep'=16,'dp'=2] {'ep'}, dimensions={0} | all-to-all | bytes 3670016 | tf_op jit(solution)/shard_map/all_to_all | solution.py:74
  412.5 0.0 copy-done.3
  412.5 0.5 fusion.15
  412.9 0.0 copy-start.4
  413.0 0.1 fusion.16
  413.1 7.3 %all_to_all.79 = bf16[16,2,1792]{2,0,1:T(8,128)(2,1)S(1)} all-to-all(bf16[16,2,1792]{2,0,1:T(8,128)(2,1)S(1)} %bitcast.55), channel_id=1, replica_groups=mesh['ep'=16,'dp'=2] {'dp'}, dimensions={1} | all-to-all | bytes 229376 | tf_op jit(solution)/shard_map/all_to_all | solution.py:86
  420.4 0.0 copy-done.5
  420.4 0.8 convolution_convert_fusion.1
  421.1 0.0 reduce-scatter.2.cloned.1.call-update
  421.2 8.0 %reduce-scatter.2.cloned.1.call-done = bf16[16,16]{1,0:T(8,128)(2,1)} async-done(((bf16[32,16]{1,0:T(8,128)(2,1)}), bf16[16,16]{1,0:T(8,128)(2,1)}) %reduce-scatter.2.cloned.1.call-update) | async-done | bytes 528 | tf_op jit(solution)/shard_map/reduce_scatter | solution.py:88
  429.2 1.3 add_divide_fusion
  430.5 0.0 copy-done.4
  430.5 0.0 copy-done.1
  (10 shorter events, 0.1 us)
Async XLA Ops:
  7.2 2.0 copy-start
  7.2 14.5 %copy-start.6 = (s32[1,224]{1,0:T(1,128)S(1)}, s32[1,224]{1,0:T(1,128)}, u32[]{:S(2)}) copy-start(s32[1,224]{1,0:T(1,128)} %param.14) | copy-start | bytes 2692
  14.3 43.8 %all-to-all-start = ((bf16[16,16,3584]{2,1,0:T(8,128)(2,1)}), bf16[16,16,3584]{2,1,0:T(8,128)(2,1)S(1)}, u32[]{:S(2)}, u32[]{:S(2)}) async-start(bf16[16,16,3584]{2,1,0:T(8,128)(2,1)} %bitcast.49), calls=%async_computation | async-start | bytes 3670016 | tf_op jit(solution)/shard_map/all_to_all | solution.py:53
  62.6 27.1 %all-to-all-start.1 = ((bf16[256,2,1792]{2,0,1:T(8,128)(2,1)}), bf16[256,2,1792]{2,0,1:T(8,128)(2,1)S(1)}, u32[]{:S(2)}, u32[]{:S(2)}) async-start(bf16[256,2,1792]{2,0,1:T(8,128)(2,1)} %copy.49), calls=%async_computation.1 | async-start | bytes 3670016 | tf_op jit(solution)/shard_map/all_to_all | solution.py:52
  73.0 26.7 %copy-start.7 = (s32[1,224]{1,0:T(1,128)S(1)}, s32[1,224]{1,0:T(1,128)}, u32[]{:S(2)}) copy-start(s32[1,224]{1,0:T(1,128)} %param.15) | copy-start | bytes 2692
  89.7 142.0 %all-to-all-start.2 = ((bf16[224,128,128]{2,1,0:T(8,128)(2,1)}), bf16[224,128,128]{2,1,0:T(8,128)(2,1)}, u32[]{:S(2)}, u32[]{:S(2)}) async-start(bf16[224,128,128]{2,1,0:T(8,128)(2,1)} %broadcast_select_fusion), calls=%async_computation.2 | async-start | bytes 14680064 | tf_op jit(solution)/shard_map/all_to_all | solution.py:48
  99.4 231.3 %all-reduce.2.cloned.1.call-start = ((), (), s32[]{:S(2)}) async-start(), calls=%async_computation.7 | async-start | bytes 2097152 | tf_op jit(solution)/shard_map/psum | solution.py:62
  252.5 6.1 %copy-start.2 = (bf16[512,14,128]{2,1,0:T(8,128)(2,1)S(1)}, bf16[512,14,128]{2,1,0:T(8,128)(2,1)}, u32[]{:S(2)}) copy-start(bf16[512,14,128]{2,1,0:T(8,128)(2,1)} %reshape.175) | copy-start | bytes 5505028
  263.7 165.5 %reduce-scatter.2.cloned.1.call-start = ((), (), s32[]{:S(2)}) async-start(), calls=%async_computation.8 | async-start | bytes 12288 | tf_op jit(solution)/shard_map/reduce_scatter | solution.py:88
  361.9 50.5 %copy-start.3 = (bf16[16,3584]{1,0:T(8,128)(2,1)S(1)}, bf16[16,3584]{1,0:T(8,128)(2,1)}, u32[]{:S(2)}) copy-start(bf16[16,3584]{1,0:T(8,128)(2,1)} %param.8) | copy-start | bytes 344068
  361.9 68.5 %copy-start.1 = (bf16[3584,16]{0,1:T(8,128)(2,1)S(1)}, bf16[3584,16]{0,1:T(8,128)(2,1)}, u32[]{:S(2)}) copy-start(bf16[3584,16]{0,1:T(8,128)(2,1)} %param.10) | copy-start | bytes 344068
  364.1 56.3 %copy-start.5 = (bf16[1792,16]{0,1:T(8,128)(2,1)S(1)}, bf16[1792,16]{0,1:T(8,128)(2,1)}, u32[]{:S(2)}) copy-start(bf16[1792,16]{0,1:T(8,128)(2,1)} %param.11) | copy-start | bytes 172036
  412.9 17.5 %copy-start.4 = (bf16[16,3584]{1,0:T(8,128)(2,1)}, bf16[16,3584]{1,0:T(8,128)(2,1)S(1)}, u32[]{:S(2)}) copy-start(bf16[16,3584]{1,0:T(8,128)(2,1)S(1)} %get-tuple-element.9) | copy-start | bytes 344068
Sparse Core Ops, SparseCore 0:
  263.8 66.7 all-reduce.1
  421.3 7.8 reduce-scatter.1
where the time goes:
time: 438 us; the launch traced here: 437 us
  waiting for transfers between devices  242 us (55%)
  blocking collectives  80.3 us (18%)
  local copies, waits for them, and re-layouts  54.6 us (12%)
  starting transfers between devices  21 us (5%)
  matrix products  15.1 us (3%)
  between operations  14.2 us (3%)
  other arithmetic  10.1 us (2%)
    all_to_all x1, waiting for transfers between devices, per_device(): lax.all_to_all(leaving, 'ep', split_axis=0, concat_axis=0, tiled=True)  130 us
    psum x1, waiting for transfers between devices, per_device(): lax.psum(product.reshape(count, hidden_width).astype(jnp.bfloat16), 'dp')  62.6 us
    all_to_all x1, blocking collectives, per_device(): lax.all_to_all(lax.all_to_all(result, 'dp', split_axis=0, concat_axis=1,...  48.3 us
    all_to_all x1, waiting for transfers between devices, per_device(): lax.all_to_all(outgoing, 'ep', split_axis=0, concat_axis=0, tiled=True)  24.9 us
    all_to_all x1, blocking collectives, per_device(): lax.all_to_all(result, 'dp', split_axis=0, concat_axis=1, tiled=True)  24.7 us
    all_to_all x1, waiting for transfers between devices, per_device(): lax.all_to_all(lax.all_to_all(outgoing, 'ep', split_axis=0, concat_axis=0...  16.8 us
    gather x1, local copies, waits for them, and re-layouts, per_device(): owned[jnp.maximum(wanted, 0)]  11.5 us
    gather x1, local copies, waits for them, and re-layouts, per_device(): arrived[cache_map.reshape(-1)]  11.4 us
  transfers between devices with their start and end apart: 5, of which 5 were waited for; matrix products, arithmetic and copies ran while one was open for 6% of the time, Pallas kernels for 0%

commit v1 on v0

--- a/solution.py
+++ b/solution.py
@@ -1,7 +1,16 @@
+import functools
 import jax
 import jax.numpy as jnp
 from jax import lax
 from jax.sharding import PartitionSpec as P
+
+
+def heads_form(chunk, row_axis):
+    x_next = jnp.sum(jax.lax.all_gather(chunk, axis_name=row_axis), axis=0)
+    return x_next
+
+
+track_fields = functools.partial(heads_form, row_axis="dp")
 
 
 def per_device(tokens, norm_gain, router, next_router, expert_ids, store, send_list, cache_map):
@@ -59,7 +68,7 @@
     count = rows.shape[0]
     block = rows.reshape(count, row_tiles, tile_rows)
     product = jnp.einsum("nat,acts->ncs", block, up_tiles, preferred_element_type=jnp.float32)
-    summed = lax.psum(product.reshape(count, hidden_width).astype(jnp.bfloat16), "dp").astype(
+    summed = track_fields(product.reshape(count, hidden_width).astype(jnp.bfloat16)).astype(
         jnp.float32
     )
     hidden = jax.nn.silu(summed).astype(jnp.bfloat16)

time: 438 us -> 434 us (level)
  waiting for transfers between devices: 242 us -> 235 us
    psum x1 -> x0, waiting for transfers between devices: 62.6 us -> none  [per_device(): lax.psum(product.reshape(count, hidden_width).astype(jnp.bfloat16), 'dp')]
    all_gather x0 -> x1, waiting for transfers between devices: none -> 55.6 us  [heads_form(): x_next = jnp.sum(jax.lax.all_gather(chunk, axis_name=row_axis), axis=0)]
where the time goes in v1:
time: 434 us; the launch traced here: 433 us
  waiting for transfers between devices  235 us (54%)
  blocking collectives  80.3 us (19%)
  local copies, waits for them, and re-layouts  55.1 us (13%)
  starting transfers between devices  21 us (5%)
  matrix products  14.5 us (3%)
  between operations  14.3 us (3%)
  other arithmetic  12.9 us (3%)
    all_to_all x1, waiting for transfers between devices, per_device(): lax.all_to_all(leaving, 'ep', split_axis=0, concat_axis=0, tiled=True)  130 us
    all_gather x1, waiting for transfers between devices, heads_form(): x_next = jnp.sum(jax.lax.all_gather(chunk, axis_name=row_axis), axis=0)  55.6 us
    all_to_all x1, blocking collectives, per_device(): lax.all_to_all(lax.all_to_all(result, 'dp', split_axis=0, concat_axis=1,...  48.3 us
    all_to_all x1, waiting for transfers between devices, per_device(): lax.all_to_all(outgoing, 'ep', split_axis=0, concat_axis=0, tiled=True)  24.9 us
    all_to_all x1, blocking collectives, per_device(): lax.all_to_all(result, 'dp', split_axis=0, concat_axis=1, tiled=True)  24.7 us
    all_to_all x1, waiting for transfers between devices, per_device(): lax.all_to_all(lax.all_to_all(outgoing, 'ep', split_axis=0, concat_axis=0...  16.8 us
    gather x1, local copies, waits for them, and re-layouts, per_device(): owned[jnp.maximum(wanted, 0)]  11.5 us
    gather x1, local copies, waits for them, and re-layouts, per_device(): arrived[cache_map.reshape(-1)]  11.4 us
  transfers between devices with their start and end apart: 5, of which 5 were waited for; matrix products, arithmetic and copies ran while one was open for 6% of the time, Pallas kernels for 0%

profile of v1, /device:TPU:0, one launch (start us, length us, event | category | flops | bytes accessed | tf_op | source)
XLA Modules:
  0.0 433.1 jit_solution(796962246271001310)
XLA Ops:
  7.2 0.0 copy-start
  7.2 0.0 copy-start.6
  7.2 1.1 fusion.14
  8.3 0.8 copy.46
  9.0 0.1 eq.36
  9.1 0.0 copy-done
  9.1 1.1 fusion.11
  10.3 0.3 select_reduce_fusion.1
  10.6 0.1 fusion.17
  10.7 0.2 reduce_window_sum.11
  10.9 0.2 select_reduce_fusion.3
  11.0 0.1 convert_element_type.96
  11.1 0.1 fusion.22
  11.2 0.2 select_reduce_fusion
  11.4 2.9 convolution_convert_fusion
  14.3 7.4 %all-to-all-start = ((bf16[16,16,3584]{2,1,0:T(8,128)(2,1)}), bf16[16,16,3584]{2,1,0:T(8,128)(2,1)S(1)}, u32[]{:S(2)}, u32[]{:S(2)}) async-start(bf16[16,16,3584]{2,1,0:T(8,128)(2,1)} %bitcast.45), calls=%async_computation | async-start | bytes 3670016 | tf_op jit(solution)/shard_map/all_to_all | solution.py:62
  21.7 0.0 copy-done.6
  21.8 11.5 %gather_fusion = bf16[224,128,128]{2,1,0:T(8,128)(2,1)} fusion(bf16[224,128,128]{2,1,0:T(8,128)(2,1)} %bitcast.46, s32[1024]{0:T(1024)S(1)} %pad_clamp_fusion.1), kind=kCustom, calls=%fused_computation | custom fusion | bytes 14680960 | tf_op jit(solution)/shard_map/gather | solution.py:55
  33.2 24.9 %all-to-all-done = bf16[16,16,3584]{2,1,0:T(8,128)(2,1)S(1)} async-done(((bf16[16,16,3584]{2,1,0:T(8,128)(2,1)}), bf16[16,16,3584]{2,1,0:T(8,128)(2,1)S(1)}, u32[]{:S(2)}, u32[]{:S(2)}) %all-to-all-start) | async-done | bytes 1835040 | tf_op jit(solution)/shard_map/all_to_all | solution.py:62
  58.1 1.5 all_to_all.57
  59.6 3.0 copy.49
  62.6 3.7 all-to-all-start.1
  66.3 6.6 %broadcast_select_fusion = bf16[224,128,128]{2,1,0:T(8,128)(2,1)} fusion(bf16[224,128,128]{2,1,0:T(8,128)(2,1)} %gather_fusion, pred[224]{0:T(512)(128)(4,1)S(1)} %compare_reduce_fusion), kind=kLoop, calls=%fused_computation.2 | loop fusion | flops 3670016 | bytes 14680288 | tf_op jit(solution)/shard_map/jit(_where)/select_n | solution.py:54
  73.0 0.0 copy-start.7
  73.0 16.8 %all-to-all-done.1 = bf16[256,2,1792]{2,0,1:T(8,128)(2,1)S(1)} async-done(((bf16[256,2,1792]{2,0,1:T(8,128)(2,1)}), bf16[256,2,1792]{2,0,1:T(8,128)(2,1)S(1)}, u32[]{:S(2)}, u32[]{:S(2)}) %all-to-all-start.1) | async-done | bytes 1835040 | tf_op jit(solution)/shard_map/all_to_all | solution.py:61
  89.7 9.6 %all-to-all-start.2 = ((bf16[224,128,128]{2,1,0:T(8,128)(2,1)}), bf16[224,128,128]{2,1,0:T(8,128)(2,1)}, u32[]{:S(2)}, u32[]{:S(2)}) async-start(bf16[224,128,128]{2,1,0:T(8,128)(2,1)} %broadcast_select_fusion), calls=%async_computation.2 | async-start | bytes 14680064 | tf_op jit(solution)/shard_map/all_to_all | solution.py:57
  99.4 0.2 all-gather.3.cloned.1.call-start
  99.6 0.0 copy-done.7
  99.6 2.4 reshape.181
  102.1 129.6 %all-to-all-done.2 = bf16[224,128,128]{2,1,0:T(8,128)(2,1)} async-done(((bf16[224,128,128]{2,1,0:T(8,128)(2,1)}), bf16[224,128,128]{2,1,0:T(8,128)(2,1)}, u32[]{:S(2)}, u32[]{:S(2)}) %all-to-all-start.2) | async-done | bytes 7340064 | tf_op jit(solution)/shard_map/all_to_all | solution.py:57
  231.7 11.4 %gather_fusion.1 = bf16[224,128,128]{2,1,0:T(8,128)(2,1)} fusion(bf16[224,128,128]{2,1,0:T(8,128)(2,1)} %all-to-all-done.2, s32[1024]{0:T(1024)S(1)} %pad_clamp_fusion), kind=kCustom, calls=%fused_computation.1 | custom fusion | bytes 14680960 | tf_op jit(solution)/shard_map/gather | solution.py:58
  243.1 9.4 %fusion.23 = (bf16[112,128,128]{2,1,0:T(8,128)(2,1)}, bf16[112,128,128]{2,1,0:T(8,128)(2,1)}) fusion(bf16[224,128,128]{2,1,0:T(8,128)(2,1)} %gather_fusion.1), kind=kLoop, calls=%fused_computation.53 | loop fusion | bytes 14680064 | tf_op jit(solution)/shard_map/slice | solution.py:60
  252.5 0.0 copy-start.2
  252.5 6.1 %copy.51 = bf16[14,8,128,128]{2,3,1,0:T(8,128)(2,1)} copy(bf16[14,8,128,128]{3,2,1,0:T(8,128)(2,1)} %bitcast.41) | data formatting | bytes 7340032 | tf_op jit(solution)/shard_map/squeeze | solution.py:59
  258.6 0.0 copy-done.2
  258.6 5.1 %bitcast_convert_fusion.1 = bf16[512,1024]{1,0:T(8,128)(2,1)} fusion(bf16[1024,14,128]{2,0,1:T(8,128)(2,1)} %bitcast.48, bf16[512,14,128]{2,1,0:T(8,128)(2,1)S(1)} %copy-done.2), kind=kOutput, calls=%fused_computation.13 | convolution fusion | flops 1879572480 | bytes 6553600 | tf_op jit(solution)/shard_map/nat,acts->ncs/dot_general | solution.py:70
  263.7 0.0 all-gather.3.cloned.1.call-update
  263.7 0.0 reduce-scatter.2.cloned.1.call-start
  263.8 4.3 %copy.54 = bf16[14,8,128,128]{3,2,0,1:T(8,128)(2,1)} copy(bf16[14,8,128,128]{3,2,1,0:T(8,128)(2,1)} %bitcast.40) | data formatting | bytes 7340032 | tf_op jit(solution)/shard_map/squeeze | solution.py:60
  268.1 55.6 %all-gather.3.cloned.1.call-done = bf16[1024,1024]{1,0:T(8,128)(2,1)} async-done(((bf16[512,1024]{1,0:T(8,128)(2,1)}), bf16[1024,1024]{1,0:T(8,128)(2,1)}) %all-gather.3.cloned.1.call-update) | async-done | bytes 2097168 | tf_op jit(solution)/shard_map/all_gather | solution.py:9
  323.7 2.2 reduce_sum.81
  325.9 0.6 fusion.4
  326.5 0.5 copy.53
  327.0 4.2 bitcast_convert_fusion
  331.2 24.7 %all_to_all.77 = bf16[2,256,1792]{2,1,0:T(8,128)(2,1)S(1)} all-to-all(bf16[2,256,1792]{2,1,0:T(8,128)(2,1)S(1)} %bitcast.50), channel_id=1, replica_groups=mesh['ep'=16,'dp'=2] {'dp'}, dimensions={0} | all-to-all | bytes 3670016 | tf_op jit(solution)/shard_map/all_to_all | solution.py:84
  355.9 1.9 copy.56
  357.7 0.0 copy-start.3
  357.8 0.0 copy-start.1
  357.8 2.2 all_to_all.64
  359.9 0.0 copy-start.5
  359.9 48.3 %all_to_all.78 = bf16[16,16,3584]{2,1,0:T(8,128)(2,1)S(1)} all-to-all(bf16[16,16,3584]{2,1,0:T(8,128)(2,1)} %all_to_all.64), channel_id=1, replica_groups=mesh['ep'=16,'dp'=2] {'ep'}, dimensions={0} | all-to-all | bytes 3670016 | tf_op jit(solution)/shard_map/all_to_all | solution.py:83
  408.3 0.0 copy-done.3
  408.3 0.5 fusion.12
  408.7 0.0 copy-start.4
  408.8 0.1 fusion.13
  408.9 7.3 %all_to_all.79 = bf16[16,2,1792]{2,0,1:T(8,128)(2,1)S(1)} all-to-all(bf16[16,2,1792]{2,0,1:T(8,128)(2,1)S(1)} %bitcast.53), channel_id=1, replica_groups=mesh['ep'=16,'dp'=2] {'dp'}, dimensions={1} | all-to-all | bytes 229376 | tf_op jit(solution)/shard_map/all_to_all | solution.py:95
  416.2 0.0 copy-done.5
  416.2 0.8 convolution_convert_fusion.1
  417.0 0.0 reduce-scatter.2.cloned.1.call-update
  417.0 8.0 %reduce-scatter.2.cloned.1.call-done = bf16[16,16]{1,0:T(8,128)(2,1)} async-done(((bf16[32,16]{1,0:T(8,128)(2,1)}), bf16[16,16]{1,0:T(8,128)(2,1)}) %reduce-scatter.2.cloned.1.call-update) | async-done | bytes 528 | tf_op jit(solution)/shard_map/reduce_scatter | solution.py:97
  425.0 1.3 add_divide_fusion
  426.3 0.0 copy-done.4
  426.3 0.0 copy-done.1
  (10 shorter events, 0.1 us)
Async XLA Ops:
  7.2 2.0 copy-start
  7.2 14.5 %copy-start.6 = (s32[1,224]{1,0:T(1,128)S(1)}, s32[1,224]{1,0:T(1,128)}, u32[]{:S(2)}) copy-start(s32[1,224]{1,0:T(1,128)} %param.14) | copy-start | bytes 2692
  14.3 43.8 %all-to-all-start = ((bf16[16,16,3584]{2,1,0:T(8,128)(2,1)}), bf16[16,16,3584]{2,1,0:T(8,128)(2,1)S(1)}, u32[]{:S(2)}, u32[]{:S(2)}) async-start(bf16[16,16,3584]{2,1,0:T(8,128)(2,1)} %bitcast.45), calls=%async_computation | async-start | bytes 3670016 | tf_op jit(solution)/shard_map/all_to_all | solution.py:62
  62.6 27.1 %all-to-all-start.1 = ((bf16[256,2,1792]{2,0,1:T(8,128)(2,1)}), bf16[256,2,1792]{2,0,1:T(8,128)(2,1)S(1)}, u32[]{:S(2)}, u32[]{:S(2)}) async-start(bf16[256,2,1792]{2,0,1:T(8,128)(2,1)} %copy.49), calls=%async_computation.1 | async-start | bytes 3670016 | tf_op jit(solution)/shard_map/all_to_all | solution.py:61
  73.0 26.7 %copy-start.7 = (s32[1,224]{1,0:T(1,128)S(1)}, s32[1,224]{1,0:T(1,128)}, u32[]{:S(2)}) copy-start(s32[1,224]{1,0:T(1,128)} %param.15) | copy-start | bytes 2692
  89.7 142.0 %all-to-all-start.2 = ((bf16[224,128,128]{2,1,0:T(8,128)(2,1)}), bf16[224,128,128]{2,1,0:T(8,128)(2,1)}, u32[]{:S(2)}, u32[]{:S(2)}) async-start(bf16[224,128,128]{2,1,0:T(8,128)(2,1)} %broadcast_select_fusion), calls=%async_computation.2 | async-start | bytes 14680064 | tf_op jit(solution)/shard_map/all_to_all | solution.py:57
  99.4 224.3 %all-gather.3.cloned.1.call-start = ((), (), s32[]{:S(2)}) async-start(), calls=%async_computation.8 | async-start | bytes 3145728 | tf_op jit(solution)/shard_map/all_gather | solution.py:9
  252.5 6.1 %copy-start.2 = (bf16[512,14,128]{2,1,0:T(8,128)(2,1)S(1)}, bf16[512,14,128]{2,1,0:T(8,128)(2,1)}, u32[]{:S(2)}) copy-start(bf16[512,14,128]{2,1,0:T(8,128)(2,1)} %reshape.181) | copy-start | bytes 5505028
  263.7 161.2 %reduce-scatter.2.cloned.1.call-start = ((), (), s32[]{:S(2)}) async-start(), calls=%async_computation.7 | async-start | bytes 12288 | tf_op jit(solution)/shard_map/reduce_scatter | solution.py:97
  357.7 50.5 %copy-start.3 = (bf16[16,3584]{1,0:T(8,128)(2,1)S(1)}, bf16[16,3584]{1,0:T(8,128)(2,1)}, u32[]{:S(2)}) copy-start(bf16[16,3584]{1,0:T(8,128)(2,1)} %param.8) | copy-start | bytes 344068
  357.8 68.5 %copy-start.1 = (bf16[3584,16]{0,1:T(8,128)(2,1)S(1)}, bf16[3584,16]{0,1:T(8,128)(2,1)}, u32[]{:S(2)}) copy-start(bf16[3584,16]{0,1:T(8,128)(2,1)} %param.10) | copy-start | bytes 344068
  359.9 56.3 %copy-start.5 = (bf16[1792,16]{0,1:T(8,128)(2,1)S(1)}, bf16[1792,16]{0,1:T(8,128)(2,1)}, u32[]{:S(2)}) copy-start(bf16[1792,16]{0,1:T(8,128)(2,1)} %param.11) | copy-start | bytes 172036
  408.7 17.5 %copy-start.4 = (bf16[16,3584]{1,0:T(8,128)(2,1)}, bf16[16,3584]{1,0:T(8,128)(2,1)S(1)}, u32[]{:S(2)}) copy-start(bf16[16,3584]{1,0:T(8,128)(2,1)S(1)} %get-tuple-element.9) | copy-start | bytes 344068
Sparse Core Ops, SparseCore 0:
  263.9 59.7 all-gather.2
  417.1 7.8 reduce-scatter.1
